TPU v7x, 256 devices: a 8x8x2 block of a 8x8x16 slice. The times are simulated.
256 devices in a mesh: groups: 2 (over z), adapter: 16 (over x, core), tensor: 8 (over y).
Axes of the slice: x: 8, y: 8, z: 2, core: 2. Of those that a mesh axis runs over, the one named last changes fastest.
The devices are a block of a 8x8x16 slice.
Arguments:
- tokens: bfloat16 [8192, 8192], P(('groups', 'adapter'), 'tensor'), parts along dimension 0, may hold values from -6 to 6
- query_weight: bfloat16 [8192, 8192], P('tensor', 'adapter'), may hold values from -0.0625 to 0.0625
- adapter_down_weight: bfloat16 [512, 16, 8192], P('adapter', None, 'tensor'), may hold values from -0.0625 to 0.0625
- adapter_up_weight: bfloat16 [512, 16, 8192], P('adapter'), may hold values from -1.5 to 1.5
- block_adapter_ids: int32 [64], P('groups'), parts along dimension 0, may hold values from 0 to 511, as said below
- block_live_count: int32 [64], P('groups'), parts along dimension 0, may hold values from 1 to 128
- adapter_slot_index: int32 [1024], P('groups'), parts along dimension 0, may hold values from 0 to 511, as said below
Outputs:
- query: bfloat16 [8192, 8192], P(('groups', 'tensor'), 'adapter'), parts along dimension 0
There are 2 independent parts, one for each index of `groups`. A program takes and returns all parts, laid end to end along the dimension named above; an argument that names none is the same for every part. Nothing has to cross between parts.
Inputs may be any that keep to these rules, and one draw needn't show every extreme that they name: Counting blocks by the owner range adapter_slot_index[block_adapter_ids[k]] // 32, no owner has more than 4 blocks, and one owner has exactly 4 in every draw. `adapter_slot_index`: A permutation: each slot holds exactly one adapter.
All inputs are finite; a program needn't handle non-finite values.
Results may differ from a plain program's by a relative error of at most 0.014.
Values may be sent and summed in bfloat16 or wider, within the bound.
A program may use at most 128 MiB of HBM per device.

v0:
```python
import jax
import jax.numpy as jnp
from jax import lax
from jax.sharding import PartitionSpec as P

BLOCK = 128


adapter_scale = 2.0


def block_plan(block_adapter_ids, adapter_slot_index, owners, adapters_per_device, capacity):
    adapters = adapter_slot_index.shape[0]
    picked = block_adapter_ids[:, None] == jnp.arange(adapters, dtype=jnp.int32)[None, :]
    block_slot_index = jnp.sum(jnp.where(picked, adapter_slot_index[None, :], 0), axis=1)
    owner_of = block_slot_index // adapters_per_device
    local_slot = block_slot_index % adapters_per_device
    hit_table = (owner_of[:, None] == jnp.arange(owners, dtype=jnp.int32)[None, :]).astype(
        jnp.int32
    )
    before = jnp.cumsum(hit_table, axis=0) - hit_table
    order_in = jnp.sum(before * hit_table, axis=1)
    return (owner_of, local_slot, order_in, owner_of * capacity + order_in)


def on_device(
    tokens,
    query_weight,
    adapter_down_weight,
    adapter_up_weight,
    block_adapter_ids,
    block_live_count,
    adapter_slot_index,
):
    owners = lax.axis_size("adapter")
    my_index = lax.axis_index("adapter")
    tok_dev = tokens.shape[0]
    features = tokens.shape[1]
    adapters_per_device = adapter_down_weight.shape[0]
    rank_width = adapter_down_weight.shape[1]
    blocks = block_adapter_ids.shape[0]
    blk_dev = blocks // owners
    capacity = 2 * blk_dev
    token_row_count = tok_dev * owners
    output_columns = query_weight.shape[1]
    owner_of, local_slot, order_in, packed = block_plan(
        block_adapter_ids, adapter_slot_index, owners, adapters_per_device, capacity
    )
    seat_ids = jnp.arange(capacity, dtype=jnp.int32)
    matches = (owner_of[None, :] == my_index) & (order_in[None, :] == seat_ids[:, None])
    filled = jnp.any(matches, axis=1)
    match_int = matches.astype(jnp.int32)
    local_adapter_rows = jnp.sum(match_int * local_slot[None, :], axis=1)
    token_keep_mask = filled.astype(jnp.bfloat16)
    positions = jnp.arange(BLOCK, dtype=jnp.int32)
    up_weight_packed = (
        jnp.take(adapter_up_weight, local_adapter_rows, axis=0) * token_keep_mask[:, None, None]
    )
    up_recv = lax.all_to_all(up_weight_packed, "adapter", split_axis=2, concat_axis=0, tiled=True)
    down_weight_packed = (
        jnp.take(adapter_down_weight, local_adapter_rows, axis=0) * token_keep_mask[:, None, None]
    )
    down_all = lax.all_gather(down_weight_packed, "adapter", axis=0, tiled=True)
    own_packed = lax.dynamic_slice_in_dim(packed, my_index * blk_dev, blk_dev)
    own_live = lax.dynamic_slice_in_dim(block_live_count, my_index * blk_dev, blk_dev)
    down_own = jnp.take(down_all, own_packed, axis=0)
    live_own = (positions[None, :] < own_live[:, None]).astype(jnp.float32)
    shrunk_own = jnp.einsum(
        "ksd,krd->ksr",
        tokens.reshape(blk_dev, BLOCK, features),
        down_own,
        preferred_element_type=jnp.float32,
    )
    shrunk_own = (
        (shrunk_own * live_own[:, :, None]).astype(jnp.bfloat16).reshape(tok_dev, rank_width)
    )
    token_piece = lax.all_gather(tokens, "adapter", axis=0, tiled=True)
    shrunk_piece = lax.all_gather(shrunk_own, "adapter", axis=0, tiled=True)
    query_product = jnp.dot(token_piece, query_weight, preferred_element_type=jnp.float32)
    up_weight_blocks = jnp.take(up_recv, packed, axis=0)
    adapter_output = jnp.einsum(
        "ksr,krf->ksf",
        shrunk_piece.reshape(blocks, BLOCK, rank_width),
        up_weight_blocks,
        preferred_element_type=jnp.float32,
    )
    partial_output = query_product + adapter_scale * adapter_output.reshape(
        token_row_count, output_columns
    )
    summed = lax.psum_scatter(
        partial_output.astype(jnp.bfloat16), "tensor", scatter_dimension=0, tiled=True
    )
    return summed


def solution(mesh):
    placed = (
        P(("groups", "adapter"), "tensor"),
        P("tensor", "adapter"),
        P("adapter", None, "tensor"),
        P("adapter", None, None),
        P("groups"),
        P("groups"),
        P("groups"),
    )
    return jax.shard_map(
        on_device,
        mesh=mesh,
        in_specs=placed,
        out_specs=P(("groups", "tensor"), "adapter"),
        check_vma=False,
    )
```

profile of v0, /device:TPU:513, one launch (start us, length us, event | category | flops | bytes accessed | tf_op | source)
XLA Modules:
  0.0 212.7 jit_solution(3576047556961893171)
XLA Ops:
  6.6 1.0 select_reduce_fusion
  7.7 0.2 select_reduce_fusion.1
  7.9 0.1 fusion.13
  8.0 0.1 select_reduce_fusion.2
  8.1 1.8 gather_fusion
  9.9 0.7 select_multiply_fusion.1
  10.8 0.7 all-gather.3.cloned.1.call-update
  11.6 4.0 %gather_fusion.2 = bf16[4,16,8192]{2,1,0:T(8,128)(2,1)S(1)} fusion(bf16[32,16,8192]{2,1,0:T(8,128)(2,1)} %param.10, s32[1024]{0:T(1024)S(1)} %pad_clamp_fusion.2), kind=kCustom, calls=%fused_computation.2 | custom fusion | bytes 2097168 | tf_op jit(solution)/shard_map/jit(_take)/gather | solution.py:57
  15.6 0.2 select_multiply_fusion
  15.7 8.3 %copy.23 = bf16[4,16,8192]{1,0,2:T(4,128)(2,1)} copy(bf16[4,16,8192]{2,1,0:T(8,128)(2,1)S(1)} %select_multiply_fusion) | data formatting | bytes 2097152 | tf_op jit(solution)/shard_map/mul | solution.py:57
  24.0 11.2 %reshape.207 = bf16[16,2,16384]{2,1,0:T(2,128)(2,1)} reshape(bf16[8192,4,16]{2,1,0:T(4,128)(2,1)} %bitcast.48) | data formatting | bytes 2097152
  35.3 23.9 %all-to-all-start = ((bf16[16,2,16384]{2,1,0:T(2,128)(2,1)}), bf16[16,2,16384]{2,1,0:T(2,128)(2,1)S(1)}, u32[]{:S(2)}, u32[]{:S(2)}) async-start(bf16[16,2,16384]{2,1,0:T(2,128)(2,1)} %reshape.207), calls=%async_computation | async-start | bytes 2097152 | tf_op jit(solution)/shard_map/all_to_all | solution.py:59
  59.3 0.1 compare_and_fusion.2
  59.5 27.7 %all-to-all-done = bf16[16,2,16384]{2,1,0:T(2,128)(2,1)S(1)} async-done(((bf16[16,2,16384]{2,1,0:T(2,128)(2,1)}), bf16[16,2,16384]{2,1,0:T(2,128)(2,1)S(1)}, u32[]{:S(2)}, u32[]{:S(2)}) %all-to-all-start) | async-done | bytes 1048608 | tf_op jit(solution)/shard_map/all_to_all | solution.py:59
  87.2 7.6 %reshape.208 = bf16[8192,4,16]{2,1,0:T(4,128)(2,1)} reshape(bf16[16,2,16384]{2,1,0:T(2,128)(2,1)S(1)} %all-to-all-done) | data formatting | bytes 2097152
  94.8 10.8 %copy.28 = bf16[4,16,16,512]{3,1,0,2:T(8,128)(2,1)S(1)} copy(bf16[4,16,16,512]{1,0,3,2:T(4,128)(2,1)} %bitcast.49) | data formatting | bytes 2097152 | tf_op jit(solution)/shard_map/all_to_all | solution.py:59
  105.6 0.6 gather_fusion.3
  106.2 2.2 %gather_fusion.1 = bf16[2,16,1024]{2,1,0:T(8,128)(2,1)S(1)} fusion(bf16[64,16,1024]{2,1,0:T(8,128)(2,1)} %all-gather.5.cloned.1.call-done, s32[1024]{0:T(1024)S(1)} %pad_clamp_fusion.1), kind=kCustom, calls=%fused_computation.1 | custom fusion | bytes 131080 | tf_op jit(solution)/shard_map/jit(_take)/gather | solution.py:66
  108.4 0.3 fusion.2
  108.7 17.2 %all_gather.11 = bf16[4096,16]{0,1:T(8,128)(2,1)S(1)} all-gather(bf16[256,16]{0,1:T(8,128)(2,1)S(1)} %bitcast.52), channel_id=1, replica_groups=mesh['groups'=2,'adapter'=16,'tensor'=8] {'adapter'}, dimensions={0}, use_global_device_ids=true | all-gather | bytes 139264 | tf_op jit(solution)/shard_map/all_gather | solution.py:78
  125.9 4.5 %broadcast_multiply_fusion = f32[32,128,512]{2,1,0:T(8,128)} fusion(bf16[32,16,512]{2,1,0:T(8,128)(2,1)S(1)} %gather_fusion.3, pred[32]{0:T(512)(128)(4,1)S(1)} %get-tuple-element.7, bf16[4096,16]{0,1:T(8,128)(2,1)S(1)} %all_gather.11), kind=kOutput, calls=%fused_computation.6 | convolution fusion | flops 69468160 | bytes 9044000 | tf_op jit(solution)/shard_map/ksr,krf->ksf/dot_general | solution.py:81
  130.4 9.4 %all-gather.3.cloned.1.call-done = bf16[4096,1024]{1,0:T(8,128)(2,1)} async-done(((bf16[256,1024]{1,0:T(8,128)(2,1)}), bf16[4096,1024]{1,0:T(8,128)(2,1)}) %all-gather.3.cloned.1.call-update) | async-done | bytes 8388624 | tf_op jit(solution)/shard_map/all_gather | solution.py:77
  139.8 10.7 %fusion = bf16[4096,512]{1,0:T(8,128)(2,1)} fusion(f32[32,128,512]{2,1,0:T(8,128)} %broadcast_multiply_fusion, bf16[4096,1024]{1,0:T(8,128)(2,1)} %all-gather.3.cloned.1.call-done, bf16[1024,512]{1,0:T(8,128)(2,1)S(1)} %copy-done), kind=kOutput, calls=%fused_computation.5 | convolution fusion | flops 4299161600 | bytes 22020096 | tf_op jit(solution)/shard_map/dot_general | solution.py:79
  150.6 55.6 %reduce-scatter.2.cloned.1.call-done = bf16[512,512]{1,0:T(8,128)(2,1)} async-done(((bf16[4096,512]{1,0:T(8,128)(2,1)}), bf16[512,512]{1,0:T(8,128)(2,1)}) %reduce-scatter.2.cloned.1.call-update) | async-done | bytes 524304 | tf_op jit(solution)/shard_map/reduce_scatter | solution.py:90
  (27 shorter events, 0.6 us)
Async XLA Ops:
  6.5 133.2 %copy-start = (bf16[1024,512]{1,0:T(8,128)(2,1)S(1)}, bf16[1024,512]{1,0:T(8,128)(2,1)}, u32[]{:S(2)}) copy-start(bf16[1024,512]{1,0:T(8,128)(2,1)} %param.8) | copy-start | bytes 3145732
  6.6 99.6 %all-gather.5.cloned.1.call-start = ((), (), s32[]{:S(2)}) async-start(), calls=%async_computation.3 | async-start | bytes 2228224 | tf_op jit(solution)/shard_map/all_gather | solution.py:63
  10.7 129.0 %all-gather.3.cloned.1.call-start = ((), (), s32[]{:S(2)}) async-start(), calls=%async_computation.2 | async-start | bytes 8912896 | tf_op jit(solution)/shard_map/all_gather | solution.py:77
  15.7 43.5 %copy-start.2 = (s32[32]{0:T(128)S(1)}, s32[32]{0:T(128)}, u32[]{:S(2)}) copy-start(s32[32]{0:T(128)} %param.12) | copy-start | bytes 388
  35.3 51.9 %all-to-all-start = ((bf16[16,2,16384]{2,1,0:T(2,128)(2,1)}), bf16[16,2,16384]{2,1,0:T(2,128)(2,1)S(1)}, u32[]{:S(2)}, u32[]{:S(2)}) async-start(bf16[16,2,16384]{2,1,0:T(2,128)(2,1)} %reshape.207), calls=%async_computation | async-start | bytes 2097152 | tf_op jit(solution)/shard_map/all_to_all | solution.py:59
  59.2 147.0 %reduce-scatter.2.cloned.1.call-start = ((), (), s32[]{:S(2)}) async-start(), calls=%async_computation.4 | async-start | bytes 4718592 | tf_op jit(solution)/shard_map/reduce_scatter | solution.py:90
  59.5 48.9 %copy-start.1 = (bf16[256,1024]{1,0:T(8,128)(2,1)S(1)}, bf16[256,1024]{1,0:T(8,128)(2,1)}, u32[]{:S(2)}) copy-start(bf16[256,1024]{1,0:T(8,128)(2,1)} %param.7) | copy-start | bytes 1572868
Sparse Core Ops, SparseCore 0:
  10.9 65.9 all-gather.4
  78.7 61.0 all-gather.2
  150.7 55.4 reduce-scatter.1
where the time goes:
time: 213 us
  waiting for transfers between devices  93.5 us (44%)
  local copies, waits for them, and re-layouts  46.6 us (22%)
  starting transfers between devices  24 us (11%)
  blocking collectives  17.2 us (8%)
  matrix products  15.5 us (7%)
  between operations  13.3 us (6%)
  other arithmetic  2.65 us (1%)
    reduce_scatter x1, waiting for transfers between devices, on_device(): lax.psum_scatter(partial_output.astype(jnp.bfloat16), 'tensor', scatter_d...  55.6 us
    all_to_all x1, waiting for transfers between devices, on_device(): lax.all_to_all(up_weight_packed, 'adapter', split_axis=2, concat_axis=0,...  27.7 us
    all_to_all x1, starting transfers between devices, on_device(): lax.all_to_all(up_weight_packed, 'adapter', split_axis=2, concat_axis=0,...  23.9 us
    unnamed x8, local copies, waits for them, and re-layouts  18.9 us
    all_gather x1, blocking collectives, on_device(): shrunk_piece = lax.all_gather(shrunk_own, 'adapter', axis=0, tiled=True)  17.2 us
    all_to_all x1, local copies, waits for them, and re-layouts, on_device(): lax.all_to_all(up_weight_packed, 'adapter', split_axis=2, concat_axis=0,...  10.8 us
    dot_general x1, matrix products, on_device(): jnp.dot(token_piece, query_weight, preferred_element_type=jnp.float32)  10.7 us
    all_gather x1, waiting for transfers between devices, on_device(): token_piece = lax.all_gather(tokens, 'adapter', axis=0, tiled=True)  9.36 us
  transfers between devices with their start and end apart: 4, of which 3 were waited for; matrix products, arithmetic and copies ran while one was open for 23% of the time, Pallas kernels for 0%

commit v1 on v0

v1 whole, which is shorter than its diff:
```python
import functools

import jax
import jax.numpy as jnp
from jax import lax
from jax.experimental import pallas as pl
from jax.experimental.pallas import tpu as pltpu
from jax.sharding import PartitionSpec as P

MESH = pl.DeviceIdType.MESH
BLOCK = 128
CORES = 2
SUB = 8
LX = 1
LY = 1
SEATS = 4
adapter_scale = 2.0


def kernel(
    nx, ny,
    ids, live, slots, tok_h, w_h, dn_h, up_h,
    out,
    tok, w, dn, upv, prod, sb, rb, fin,
    u1s, u1r, u2s, u2r, shq, s1s, s1r, s2s, s2r,
    tab_slot, tab_seat,
    ld_sem, xs, xr, ds, dr, ys, yr,
    u1ss, u1rs, u2ss, u2rs, s1ss, s1rs, s2ss, s2rs,
):
    S = SUB
    R, Fe = tok.shape[3], tok.shape[4]
    half = Fe // 2
    N = w.shape[1]
    slots_dev = dn.shape[0]
    HX, HY = nx // 2, ny // 2
    NT = tok.shape[0]
    nblk = ids.shape[0]
    per_row = nblk // ny
    per_dev = per_row // CORES
    lanes = upv.shape[3]
    qpc = N // lanes

    ad = lax.axis_index("adapter")
    y = lax.axis_index("tensor")
    x = lax.div(ad, CORES)
    c = lax.rem(ad, CORES)
    oc = 1 - c

    def dev(dx=0, dy=0, core=None):
        core = c if core is None else core
        return {
            "adapter": lax.rem(x + (dx + nx) % nx, nx) * CORES + core,
            "tensor": lax.rem(y + (dy + ny) % ny, ny),
        }

    def rcopy(src, dst, ssem, rsem, where):
        return pltpu.make_async_remote_copy(
            src_ref=src, dst_ref=dst, send_sem=ssem, recv_sem=rsem,
            device_id=where, device_id_type=MESH,
        )

    def load_tok(s):
        return pltpu.make_async_copy(
            tok_h.at[pl.ds(s * R, R)], tok.at[s, 0, c], ld_sem.at[s]
        )

    def load_up(i):
        return pltpu.make_async_copy(
            up_h.at[:, :, pl.ds(pl.multiple_of(i * N * CORES + y * lanes, lanes), lanes)],
            upv.at[i], ld_sem.at[S + 2 + i],
        )

    load_w = pltpu.make_async_copy(w_h, w, ld_sem.at[S])
    load_dn = pltpu.make_async_copy(dn_h, dn, ld_sem.at[S + 1])
    for s in range(S):
        load_tok(s).start()
    load_w.start()
    load_dn.start()
    for i in range(nx):
        load_up(i).start()

    barrier = pltpu.get_barrier_semaphore()
    for where in (dev(1), dev(-1), dev(0, 1), dev(0, -1), dev(0, 0, oc)):
        pl.semaphore_signal(barrier, inc=1, device_id=where, device_id_type=MESH)
    pl.semaphore_wait(barrier, 5)

    def x_copy(way, d, s):
        off = (nx - d) % nx if way == 0 else d
        noff = nx - d - 1 if way == 0 else d + 1
        t = s + LX * d
        src = tok.at[t, off, c]
        dst = tok.at[t + LX, noff, c]
        if d == HX - 1:
            cols = pl.ds(way * half, half)
            src, dst = src.at[:, cols], dst.at[:, cols]
        return rcopy(
            src, dst, xs.at[way, d, s], xr.at[way, d, s], dev(1 if way == 0 else -1)
        )

    def core_copy(off, s):
        t = s + LX * min(off, nx - off)
        return rcopy(
            tok.at[t, off, c], tok.at[t, off, c], ds.at[off, s], dr.at[off, s],
            dev(0, 0, oc),
        )

    def core_wait(off, s):
        t = s + LX * min(off, nx - off)
        rcopy(
            tok.at[t, off, oc], tok.at[t, off, oc], ds.at[off, s], dr.at[off, s],
            dev(0, 0, oc),
        ).wait_recv()

    def own_send(s):
        load_tok(s).wait()
        x_copy(0, 0, s).start()
        x_copy(1, 0, s).start()
        core_copy(0, s).start()

    def y_copy(way, d, s):
        src, dst = sb.at[way, d - 1, s], rb.at[way, d - 1, s]
        if d == HY:
            src, dst = src.at[pl.ds(0, R)], dst.at[pl.ds(0, R)]
        return rcopy(
            src, dst, ys.at[way, d - 1, s], yr.at[way, d - 1, s],
            dev(0, 1 if way == 0 else -1),
        )

    own_send(0)

    def plan(k, seats):
        slot = slots[ids[k]]
        owner = lax.div(slot, slots_dev)
        tab_slot[k] = slot

        def count(i, n):
            return n + jnp.where(lax.div(tab_slot[i], slots_dev) == owner, 1, 0)

        seat = lax.fori_loop(0, k, count, jnp.int32(0))
        seat = jnp.minimum(seat, SEATS - 1)
        tab_seat[k] = seat
        mine = owner == ad
        return tuple(
            jnp.where(mine & (seat == q), k, seats[q]) for q in range(SEATS)
        )

    seat_blk = lax.fori_loop(0, nblk, plan, (jnp.int32(0),) * SEATS)

    load_w.wait()

    def u1_copy(i):
        return rcopy(u1s.at[i], u1r.at[i], u1ss.at[i], u1rs.at[i], dev(i))

    def up_first():
        for i in range(nx):
            load_up(i).wait()
        for q in range(SEATS):
            row = lax.rem(tab_slot[seat_blk[q]], slots_dev)
            for i in range(nx):
                v = upv[lax.rem(x + i, nx), row]
                if i == 0:
                    u1r[0, q] = v
                else:
                    u1s[i, q] = v
        for i in range(1, nx):
            u1_copy(i).start()

    dest_core = lax.div(y, qpc)
    y_in = lax.rem(y, qpc)

    def u2_copy(i):
        return rcopy(
            u2s.at[i], u2r.at[c, y_in], u2ss.at[i], u2rs.at[c, y_in],
            dev(0, i, dest_core),
        )

    def up_second():
        for i in range(1, nx):
            u1_copy(i).wait_recv()
        for i in range(ny):
            row = lax.rem(y + i, ny)
            for b in range(per_row):
                k = row * per_row + b
                owner = lax.div(tab_slot[k], slots_dev)
                rel = lax.rem(x - lax.div(owner, CORES) + nx, nx)
                v = u1r[rel, tab_seat[k]]
                keep = lax.rem(owner, CORES) == c
                u2s[i, b] = jnp.where(keep, v, jnp.zeros_like(v))
        for i in range(1, ny):
            u2_copy(i).start()

        @pl.when(dest_core == c)
        def _():
            u2r[c, y_in] = u2s[0]

        @pl.when(dest_core != c)
        def _():
            u2_copy(0).start()

    def s1_copy(hr, i):
        return rcopy(
            s1s.at[hr, i], s1r.at[hr, i], s1ss.at[hr, i], s1rs.at[hr, i],
            dev(0, i, c if hr == 0 else oc),
        )

    def shrink_first():
        load_dn.wait()
        for q in range(SEATS):
            k = seat_blk[q]
            a = lax.div(k, per_dev)
            piece = lax.rem(k, per_dev)
            off = lax.rem(lax.div(a, CORES) - x + nx, nx)
            dist = jnp.minimum(off, nx - off)
            ca = lax.rem(a, CORES)
            n_sub = S // per_dev
            rows = [
                tok[piece * n_sub + i + LX * dist, off, ca] for i in range(n_sub)
            ]
            rows = jnp.concatenate(rows, axis=0) if n_sub > 1 else rows[0]
            weight = dn[lax.rem(tab_slot[k], slots_dev)]
            v = lax.dot_general(
                weight, rows, (((1,), (1,)), ((), ())),
                preferred_element_type=jnp.float32,
            )
            pos = lax.broadcasted_iota(jnp.int32, v.shape, 1)
            shq[q] = jnp.where(pos < live[k], v, 0.0).astype(shq.dtype)
        for i in range(ny):
            row = lax.rem(y + i, ny)
            for hr in range(CORES):
                h = c if hr == 0 else oc
                for b in range(per_dev):
                    k = row * per_row + h * per_dev + b
                    v = shq[tab_seat[k]]
                    v = jnp.where(
                        lax.div(tab_slot[k], slots_dev) == ad, v, jnp.zeros_like(v)
                    )
                    if hr == 0 and i == 0:
                        s1r[0, 0, b] = v
                    else:
                        s1s[hr, i, b] = v
        for i in range(ny):
            for hr in range(CORES):
                if hr or i:
                    s1_copy(hr, i).start()

    def s2_copy(hr, i):
        return rcopy(
            s2s, s2r.at[hr, i], s2ss.at[hr, i], s2rs.at[hr, i],
            dev(i, 0, c if hr == 0 else oc),
        )

    def shrink_second():
        for i in range(ny):
            for hr in range(CORES):
                if hr or i:
                    s1_copy(hr, i).wait_recv()
        v = jnp.sum(s1r[...].astype(jnp.float32), axis=(0, 1)).astype(s2s.dtype)
        s2s[...] = v
        s2r[0, 0] = v
        for i in range(nx):
            for hr in range(CORES):
                if hr or i:
                    s2_copy(hr, i).start()

    y_order = [HY]
    for d in range(HY - 1, 0, -1):
        y_order += [d, ny - d]
    y_order += [0]

    def tick(t, carry):
        for d in range(HX, 0, -1):
            s = t - LX * d

            @pl.when((s >= 0) & (s < S))
            def _(d=d, s=s):
                for way in range(2):
                    x_copy(way, d - 1, s).wait_recv()
                    if d < HX:
                        x_copy(way, d, s).start()
                if d < HX:
                    core_copy(nx - d, s).start()
                core_copy(d, s).start()

        @pl.when(t + 1 < S)
        def _():
            own_send(t + 1)

        for d in range(HX + 1):
            s = t - LX * d

            @pl.when((s >= 0) & (s < S))
            def _(d=d, s=s):
                core_wait(d, s)
                if 0 < d < HX:
                    core_wait(nx - d, s)

        @pl.when(t < NT)
        def _():
            v = jnp.dot(
                tok[t].reshape(nx * CORES * R, Fe), w[...],
                preferred_element_type=jnp.float32,
            )
            prod[t] = v.reshape(nx, CORES * R, N)

        for o in y_order:
            d = min(o, ny - o)
            way = 0 if o <= HY else 1
            off = lax.rem(lax.rem(y + o, ny) - x + nx, nx)
            dx = jnp.minimum(off, nx - off)
            s = t - LX * dx - LY * (HY - d)

            @pl.when((s >= 0) & (s < S))
            def _(o=o, d=d, way=way, off=off, dx=dx, s=s):
                v = prod.at[s + LX * dx, off]
                top, low = pl.ds(0, R), pl.ds(R, R)
                dt = sb.dtype
                if d == HY:
                    sb[0, d - 1, s, top] = v[top].astype(dt)
                    sb[1, d - 1, s, top] = v[low].astype(dt)
                    y_copy(0, d, s).start()
                    y_copy(1, d, s).start()
                elif d == HY - 1:
                    y_copy(way, d + 1, s).wait_recv()
                    got = rb[way, d, s, top].astype(jnp.float32)
                    add, keep = (top, low) if way == 0 else (low, top)
                    sb[way, d - 1, s, add] = (v[add] + got).astype(dt)
                    sb[way, d - 1, s, keep] = v[keep].astype(dt)
                    y_copy(way, d, s).start()
                elif d > 0:
                    y_copy(way, d + 1, s).wait_recv()
                    got = rb[way, d, s].astype(jnp.float32)
                    sb[way, d - 1, s] = (v[...] + got).astype(dt)
                    y_copy(way, d, s).start()
                else:
                    y_copy(0, 1, s).wait_recv()
                    y_copy(1, 1, s).wait_recv()
                    total = (
                        v[...]
                        + rb[0, 0, s].astype(jnp.float32)
                        + rb[1, 0, s].astype(jnp.float32)
                    )
                    fin[0, s] = total[:R]
                    fin[1, s] = total[R:]

        @pl.when(t == LX * HX + 1)
        def _():
            up_first()

        @pl.when(t == NT - 2)
        def _():
            up_second()

        @pl.when(t == NT - 1)
        def _():
            shrink_first()

        @pl.when(t == NT + 1)
        def _():
            shrink_second()

        return carry

    lax.fori_loop(0, NT + LY * HY, tick, 0)

    for p in range(qpc):
        for cs in range(CORES):
            own = (c == cs) & (y == c * qpc + p)

            @pl.when(jnp.logical_not(own))
            def _(cs=cs, p=p):
                rcopy(
                    u2s.at[0], u2r.at[cs, p], u2ss.at[0], u2rs.at[cs, p], dev(0, 0, oc)
                ).wait_recv()

    for i in range(nx):
        for hr in range(CORES):
            if hr or i:
                s2_copy(hr, i).wait_recv()
    ups = u2r[0] + u2r[1]
    for hr in range(CORES):
        h = c if hr == 0 else oc
        sh = s2r[hr, 0]
        for i in range(1, nx):
            sh = sh + s2r[hr, i]
        n_sub = S // per_dev
        for b in range(per_dev):
            blk = h * per_dev + b
            up = jnp.concatenate(
                [u2r[0, p, blk] + u2r[1, p, blk] for p in range(qpc)], axis=1
            )
            part = lax.dot_general(
                sh[b], up, (((0,), (0,)), ((), ())),
                preferred_element_type=jnp.float32,
            )
            base = fin[h, pl.ds(b * n_sub, n_sub)].reshape(n_sub * R, N)
            start = pl.multiple_of(h * (S * R) + b * BLOCK, BLOCK)
            out[pl.ds(start, BLOCK), :] = (base + adapter_scale * part).astype(out.dtype)

    def drain(s, carry):
        for d in range(HX):
            x_copy(0, d, s).wait_send()
            x_copy(1, d, s).wait_send()
        for off in range(nx):
            core_copy(off, s).wait_send()
        for d in range(1, HY + 1):
            y_copy(0, d, s).wait_send()
            y_copy(1, d, s).wait_send()
        return carry

    lax.fori_loop(0, S, drain, 0)
    for i in range(1, nx):
        u1_copy(i).wait_send()
    for i in range(1, ny):
        u2_copy(i).wait_send()

    @pl.when(dest_core != c)
    def _():
        u2_copy(0).wait_send()

    for i in range(ny):
        for hr in range(CORES):
            if hr or i:
                s1_copy(hr, i).wait_send()
    for i in range(nx):
        for hr in range(CORES):
            if hr or i:
                s2_copy(hr, i).wait_send()


def on_device(tokens, query_weight, down, up, ids, live, slots):
    nx = lax.axis_size("adapter") // CORES
    ny = lax.axis_size("tensor")
    rows, Fe = tokens.shape
    N = query_weight.shape[1]
    slots_dev, rank = down.shape[0], down.shape[1]
    R = rows // SUB
    NT = SUB + LX * (nx // 2)
    HX, HY = nx // 2, ny // 2
    lanes = N * CORES // ny
    qpc = N // lanes
    per_row = ids.shape[0] // ny
    per_dev = per_row // CORES
    bf = jnp.bfloat16
    dma = pltpu.SemaphoreType.DMA
    smem = pl.BlockSpec(memory_space=pltpu.SMEM)
    hbm = pl.BlockSpec(memory_space=pl.ANY)
    piece = (per_dev, rank, BLOCK)
    return pl.pallas_call(
        functools.partial(kernel, nx, ny),
        out_shape=jax.ShapeDtypeStruct((CORES * rows, N), bf),
        in_specs=[smem] * 3 + [hbm] * 4,
        out_specs=pl.BlockSpec(memory_space=pltpu.VMEM),
        scratch_shapes=[
            pltpu.VMEM((NT, nx, CORES, R, Fe), bf),
            pltpu.VMEM((Fe, N), bf),
            pltpu.VMEM((slots_dev, rank, Fe), bf),
            pltpu.VMEM((nx, slots_dev, rank, lanes), bf),
            pltpu.VMEM((NT, nx, CORES * R, N), jnp.float32),
            pltpu.VMEM((2, HY, SUB, CORES * R, N), bf),
            pltpu.VMEM((2, HY, SUB, CORES * R, N), bf),
            pltpu.VMEM((CORES, SUB, R, N), jnp.float32),
            pltpu.VMEM((nx, SEATS, rank, lanes), bf),
            pltpu.VMEM((nx, SEATS, rank, lanes), bf),
            pltpu.VMEM((ny, per_row, rank, lanes), bf),
            pltpu.VMEM((CORES, qpc, per_row, rank, lanes), bf),
            pltpu.VMEM((SEATS, rank, BLOCK), bf),
            pltpu.VMEM((CORES, ny) + piece, bf),
            pltpu.VMEM((CORES, ny) + piece, bf),
            pltpu.VMEM(piece, bf),
            pltpu.VMEM((CORES, nx) + piece, bf),
            pltpu.SMEM((ids.shape[0],), jnp.int32),
            pltpu.SMEM((ids.shape[0],), jnp.int32),
            dma((SUB + 2 + nx,)),
            dma((2, HX, SUB)), dma((2, HX, SUB)),
            dma((nx, SUB)), dma((nx, SUB)),
            dma((2, HY, SUB)), dma((2, HY, SUB)),
            dma((nx,)), dma((nx,)),
            dma((ny,)), dma((CORES, qpc)),
            dma((CORES, ny)), dma((CORES, ny)),
            dma((CORES, nx)), dma((CORES, nx)),
        ],
        compiler_params=pltpu.CompilerParams(
            collective_id=0, has_side_effects=True,
            vmem_limit_bytes=60 * 1024 * 1024,
        ),
    )(ids, live, slots, tokens, query_weight, down, up)


def solution(mesh):
    placed = (
        P(("groups", "adapter"), "tensor"),
        P("tensor", "adapter"),
        P("adapter", None, "tensor"),
        P("adapter", None, None),
        P("groups"),
        P("groups"),
        P("groups"),
    )
    return jax.shard_map(
        on_device,
        mesh=mesh,
        in_specs=placed,
        out_specs=P(("groups", "tensor"), "adapter"),
        check_vma=False,
    )
```

time: 213 us -> 108 us (0.51)
  Pallas kernels: 0 us -> 106 us
  waiting for transfers between devices: 93.5 us -> 0 us
  local copies, waits for them, and re-layouts: 46.6 us -> 1.87 us
  starting transfers between devices: 24 us -> 0 us
  blocking collectives: 17.2 us -> 0 us
  matrix products: 15.5 us -> 0 us
  between operations: 13.3 us -> 0.01 us
  other arithmetic: 2.65 us -> 0 us
    pallas_call x0 -> x1, Pallas kernels: none -> 106 us  [on_device(): pl.pallas_call(functools.partial(kernel, nx, ny), out_shape=jax.ShapeDtyp...]
    reduce_scatter x1 -> x0, waiting for transfers between devices: 55.6 us -> none  [on_device(): lax.psum_scatter(partial_output.astype(jnp.bfloat16), 'tensor', scatter_d...]
    all_to_all x1 -> x0, waiting for transfers between devices: 27.7 us -> none  [on_device(): lax.all_to_all(up_weight_packed, 'adapter', split_axis=2, concat_axis=0,...]
    all_to_all x1 -> x0, starting transfers between devices: 23.9 us -> none  [on_device(): lax.all_to_all(up_weight_packed, 'adapter', split_axis=2, concat_axis=0,...]
    all_gather x1 -> x0, blocking collectives: 17.2 us -> none  [on_device(): shrunk_piece = lax.all_gather(shrunk_own, 'adapter', axis=0, tiled=True)]
    unnamed x8 -> x1, local copies, waits for them, and re-layouts: 18.9 us -> 1.87 us
    dot_general x3 -> x0, matrix products: 15.5 us -> none  [the longest x1 10.7 us: on_device(): jnp.dot(token_piece, query_weight, preferred_element_type=jnp.float32)]
    all_to_all x1 -> x0, local copies, waits for them, and re-layouts: 10.8 us -> none  [on_device(): lax.all_to_all(up_weight_packed, 'adapter', split_axis=2, concat_axis=0,...]
  transfers between devices with their start and end apart: 4 -> 0, of which waited for: 3 -> 0; matrix products, arithmetic and copies ran while one was open for 23% -> 0% of each run, Pallas kernels for 0% -> 0%
where the time goes in v1:
time: 108 us
  Pallas kernels  106 us (98%)
  local copies, waits for them, and re-layouts  1.87 us (2%)
    pallas_call x1, Pallas kernels, on_device(): pl.pallas_call(functools.partial(kernel, nx, ny), out_shape=jax.ShapeDtyp...  106 us

profile of v1, /device:TPU:513, one launch (start us, length us, event | category | flops | bytes accessed | tf_op | source)
XLA Modules:
  0.0 107.8 jit_solution(8855941039729802554)
XLA Ops:
  0.0 106.0 %shard_map.73 = bf16[512,512]{1,0:T(8,128)(2,1)} custom-call(s32[32]{0:T(128)} %ids.1, s32[32]{0:T(128)} %live.1, s32[512]{0:T(512)} %slots.1, bf16[256,1024]{1,0:T(8,128)(2,1)} %tok_h.1, bf16[1024,512]{1,0:T(8,128)(2,1)} %w_h.1, bf16[32,16,1024]{2,1,0:T(8,128)(2,1)} %dn_h.1, bf16[32,16,8192]{2,1,0:T(8,128)(2,1)} %up_h.1), custom_call_target="tpu_custom_call" | custom-call | tf_op jit(solution)/shard_map/pallas_call | solution.py:448
  106.0 1.9 %copy.9 = bf16[512,512]{1,0:T(8,128)(2,1)} copy(bf16[512,512]{1,0:T(8,128)(2,1)} %shard_map.73) | data formatting | bytes 1048576

commit v2 on v1

v2 whole, which is shorter than its diff:
```python
import functools

import jax
import jax.numpy as jnp
from jax import lax
from jax.experimental import pallas as pl
from jax.experimental.pallas import tpu as pltpu
from jax.sharding import PartitionSpec as P

MESH = pl.DeviceIdType.MESH
BLOCK = 128
CORES = 2
SUB = 16
LX = 2
LY = 2
LAG = 2
AHEAD = 1
SEATS = 4
UP1 = 8
UP2 = 20
SH2 = 3
adapter_scale = 2.0


def kernel(
    nx, ny,
    ids, live, slots, tok_h, w_h, dn_h, up_h,
    out,
    tok, w, dn, upv, prod, sb, rb, fin,
    u1s, u1r, u2s, u2r, shq, s1s, s1r, s2s, s2r,
    tab_owner, tab_row, tab_seat,
    obuf, st_sem, ld_sem, xs, xr, ds, dr, ys, yr,
    u1ss, u1rs, u2ss, u2rs, s1ss, s1rs, s2ss, s2rs,
):
    S = SUB
    R, Fe = tok.shape[3], tok.shape[4]
    half = Fe // 2
    N = w.shape[1]
    slots_dev = dn.shape[0]
    HX, HY = nx // 2, ny // 2
    NT = tok.shape[0]
    nblk = ids.shape[0]
    per_row = nblk // ny
    per_dev = per_row // CORES
    lanes = upv.shape[3]
    qpc = N // lanes

    ad = lax.axis_index("adapter")
    y = lax.axis_index("tensor")
    x = lax.div(ad, CORES)
    c = lax.rem(ad, CORES)
    oc = 1 - c

    def dev(dx=0, dy=0, core=None):
        core = c if core is None else core
        return {
            "adapter": lax.rem(x + (dx + nx) % nx, nx) * CORES + core,
            "tensor": lax.rem(y + (dy + ny) % ny, ny),
        }

    def rcopy(src, dst, ssem, rsem, where):
        return pltpu.make_async_remote_copy(
            src_ref=src, dst_ref=dst, send_sem=ssem, recv_sem=rsem,
            device_id=where, device_id_type=MESH,
        )

    load_tok = pltpu.make_async_copy(tok_h, tok.at[pl.ds(0, S), 0, c], ld_sem.at[0])

    def load_up(i):
        return pltpu.make_async_copy(
            up_h.at[:, :, pl.ds(pl.multiple_of(i * N * CORES + y * lanes, lanes), lanes)],
            upv.at[i], ld_sem.at[3],
        )

    load_w = pltpu.make_async_copy(w_h, w, ld_sem.at[1])
    load_dn = pltpu.make_async_copy(dn_h, dn, ld_sem.at[2])
    load_tok.start()
    load_w.start()
    load_dn.start()
    for i in range(nx):
        load_up(i).start()

    barrier = pltpu.get_barrier_semaphore()
    for where in (dev(1), dev(-1), dev(0, 1), dev(0, -1), dev(0, 0, oc)):
        pl.semaphore_signal(barrier, inc=1, device_id=where, device_id_type=MESH)
    pl.semaphore_wait(barrier, 5)

    def x_copy(way, d, s):
        off = (nx - d) % nx if way == 0 else d
        noff = nx - d - 1 if way == 0 else d + 1
        t = s + LX * d
        src = tok.at[t, off, c]
        dst = tok.at[t + LX, noff, c]
        if d == HX - 1:
            cols = pl.ds(way * half, half)
            src, dst = src.at[:, cols], dst.at[:, cols]
        return rcopy(
            src, dst, xs.at[way, 1 if d == HX - 1 else 0], xr.at[way, d, s],
            dev(1 if way == 0 else -1),
        )

    def core_copy(t, core):
        part = tok.at[t, :, core]
        return rcopy(part, part, ds.at[0], dr.at[t], dev(0, 0, oc))

    def own_send(s):
        x_copy(0, 0, s).start()
        x_copy(1, 0, s).start()

    def y_copy(way, d, s):
        src, dst = sb.at[way, d - 1, s], rb.at[way, d - 1, s]
        if d == HY:
            src, dst = src.at[pl.ds(0, R)], dst.at[pl.ds(0, R)]
        return rcopy(
            src, dst, ys.at[way, 1 if d == HY else 0], yr.at[way, d - 1, s],
            dev(0, 1 if way == 0 else -1),
        )

    load_tok.wait()
    for s in range(AHEAD):
        own_send(s)

    def place(k, carry):
        slot = slots[ids[k]]
        tab_owner[k] = lax.div(slot, slots_dev)
        tab_row[k] = lax.rem(slot, slots_dev)
        return carry

    lax.fori_loop(0, nblk, place, 0)

    def plan(k, seats):
        owner = tab_owner[k]
        seat = jnp.int32(0)
        for i in range(nblk):
            seat += jnp.where((tab_owner[i] == owner) & (i < k), 1, 0)
        seat = jnp.minimum(seat, SEATS - 1)
        tab_seat[k] = seat
        mine = owner == ad
        return tuple(
            jnp.where(mine & (seat == q), k, seats[q]) for q in range(SEATS)
        )

    seat_blk = lax.fori_loop(0, nblk, plan, (jnp.int32(0),) * SEATS)

    load_w.wait()

    def u1_copy(i):
        return rcopy(u1s.at[i], u1r.at[i], u1ss.at[0], u1rs.at[0], dev(i))

    def up_first():
        pltpu.make_async_copy(upv, upv, ld_sem.at[3]).wait()
        for q in range(SEATS):
            row = tab_row[seat_blk[q]]
            for i in range(nx):
                v = upv[lax.rem(x + i, nx), row]
                if i == 0:
                    u1r[0, q] = v
                else:
                    u1s[i, q] = v
        for i in range(1, nx):
            u1_copy(i).start()

    dest_core = lax.div(y, qpc)
    y_in = lax.rem(y, qpc)

    def u2_copy(i):
        return rcopy(
            u2s.at[i], u2r.at[c, y_in], u2ss.at[min(i, 1)], u2rs.at[c, y_in],
            dev(0, i, dest_core),
        )

    def up_second():
        rest = u1r.at[pl.ds(1, nx - 1)]
        rcopy(rest, rest, u1ss.at[0], u1rs.at[0], dev(1)).wait_recv()
        for i in range(ny):
            row = lax.rem(y + i, ny)
            for b in range(per_row):
                k = row * per_row + b
                owner = tab_owner[k]
                rel = lax.rem(x - lax.div(owner, CORES) + nx, nx)
                v = u1r[rel, tab_seat[k]]
                keep = lax.rem(owner, CORES) == c
                u2s[i, b] = jnp.where(keep, v, jnp.zeros_like(v))
        for i in range(1, ny):
            u2_copy(i).start()

        @pl.when(dest_core == c)
        def _():
            u2r[c, y_in] = u2s[0]

        @pl.when(dest_core != c)
        def _():
            u2_copy(0).start()

    def s1_copy(hr, i):
        return rcopy(
            s1s.at[hr, i], s1r.at[hr, i], s1ss.at[hr], s1rs.at[hr],
            dev(0, i, c if hr == 0 else oc),
        )

    def shrink_first():
        load_dn.wait()
        for q in range(SEATS):
            k = seat_blk[q]
            a = lax.div(k, per_dev)
            piece = lax.rem(k, per_dev)
            off = lax.rem(lax.div(a, CORES) - x + nx, nx)
            dist = jnp.minimum(off, nx - off)
            ca = lax.rem(a, CORES)
            n_sub = S // per_dev
            rows = [
                tok[piece * n_sub + i + LX * dist, off, ca] for i in range(n_sub)
            ]
            rows = jnp.concatenate(rows, axis=0) if n_sub > 1 else rows[0]
            weight = dn[tab_row[k]]
            v = lax.dot_general(
                weight, rows, (((1,), (1,)), ((), ())),
                preferred_element_type=jnp.float32,
            )
            pos = lax.broadcasted_iota(jnp.int32, v.shape, 1)
            shq[q] = jnp.where(pos < live[k], v, 0.0).astype(shq.dtype)
        for i in range(ny):
            row = lax.rem(y + i, ny)
            for hr in range(CORES):
                h = c if hr == 0 else oc
                for b in range(per_dev):
                    k = row * per_row + h * per_dev + b
                    v = shq[tab_seat[k]]
                    v = jnp.where(tab_owner[k] == ad, v, jnp.zeros_like(v))
                    if hr == 0 and i == 0:
                        s1r[0, 0, b] = v
                    else:
                        s1s[hr, i, b] = v
        for i in range(ny):
            for hr in range(CORES):
                if hr or i:
                    s1_copy(hr, i).start()

    def s2_copy(hr, i):
        return rcopy(
            s2s, s2r.at[hr, i], s2ss.at[hr], s2rs.at[hr],
            dev(i, 0, c if hr == 0 else oc),
        )

    def shrink_second():
        for hr in range(CORES):
            got = s1r.at[hr, pl.ds(1 - hr, ny - 1 + hr)]
            rcopy(got, got, s1ss.at[hr], s1rs.at[hr], dev(0, 0, oc)).wait_recv()
        v = jnp.sum(s1r[...].astype(jnp.float32), axis=(0, 1)).astype(s2s.dtype)
        s2s[...] = v
        s2r[0, 0] = v
        for i in range(nx):
            for hr in range(CORES):
                if hr or i:
                    s2_copy(hr, i).start()

    def chain(o, t):
        d = min(o, ny - o)
        way = 0 if o <= HY else 1
        off = lax.rem(lax.rem(y + o, ny) - x + nx, nx)
        dx = jnp.minimum(off, nx - off)
        s = t - LX * dx - LY * (HY - d) - LAG

        @pl.when((s >= 0) & (s < S))
        def _():
            v = prod.at[s + LX * dx, off]
            top, low = pl.ds(0, R), pl.ds(R, R)
            dt = sb.dtype
            if d == HY:
                sb[0, d - 1, s, top] = v[top].astype(dt)
                sb[1, d - 1, s, top] = v[low].astype(dt)
                y_copy(0, d, s).start()
                y_copy(1, d, s).start()
            elif d == HY - 1:
                add, keep = (top, low) if way == 0 else (low, top)
                sb[way, d - 1, s, keep] = v[keep].astype(dt)
                y_copy(way, d + 1, s).wait_recv()
                got = rb[way, d, s, top].astype(jnp.float32)
                sb[way, d - 1, s, add] = (v[add] + got).astype(dt)
                y_copy(way, d, s).start()
            elif d > 0:
                y_copy(way, d + 1, s).wait_recv()
                got = rb[way, d, s].astype(jnp.float32)
                sb[way, d - 1, s] = (v[...] + got).astype(dt)
                y_copy(way, d, s).start()
            else:
                y_copy(0, 1, s).wait_recv()
                y_copy(1, 1, s).wait_recv()
                total = (
                    v[...]
                    + rb[0, 0, s].astype(jnp.float32)
                    + rb[1, 0, s].astype(jnp.float32)
                )
                fin[0, s] = total[:R]
                fin[1, s] = total[R:]

    def forward(d, t):
        s = t - LX * d

        @pl.when((s >= 0) & (s < S))
        def _():
            for way in range(2):
                x_copy(way, d - 1, s).wait_recv()
                if d < HX:
                    x_copy(way, d, s).start()

    def tick(t, carry):
        @pl.when(t == NT + SH2)
        def _():
            shrink_second()

        for k in range(max(HX, HY)):
            if k < HX:
                forward(HX - k, t)
            if k < HY:
                for o in sorted({HY - k, ny - HY + k}):
                    chain(o, t)

        @pl.when(t + AHEAD < S)
        def _():
            own_send(t + AHEAD)

        chain(0, t)

        @pl.when(t < NT)
        def _():
            core_copy(t, c).start()

        @pl.when((t >= 1) & (t <= NT))
        def _():
            core_copy(t - 1, oc).wait_recv()
            v = jnp.dot(
                tok[t - 1].reshape(nx * CORES * R, Fe), w[...],
                preferred_element_type=jnp.float32,
            )
            prod[t - 1] = v.reshape(nx, CORES * R, N)

        @pl.when(t == UP1)
        def _():
            up_first()

        @pl.when(t == UP2)
        def _():
            up_second()

        @pl.when(t == NT)
        def _():
            shrink_first()

        return carry

    lax.fori_loop(0, NT + LY * HY + LAG, tick, 0)

    for p in range(qpc):
        for cs in range(CORES):
            own = (c == cs) & (y == c * qpc + p)

            @pl.when(jnp.logical_not(own))
            def _(cs=cs, p=p):
                rcopy(
                    u2s.at[0], u2r.at[cs, p], u2ss.at[0], u2rs.at[cs, p], dev(0, 0, oc)
                ).wait_recv()

    for hr in range(CORES):
        got = s2r.at[hr, pl.ds(1 - hr, nx - 1 + hr)]
        rcopy(got, got, s2ss.at[hr], s2rs.at[hr], dev(0, 0, oc)).wait_recv()
    stores = []
    for hr in range(CORES):
        h = c if hr == 0 else oc
        sh = s2r[hr, 0]
        for i in range(1, nx):
            sh = sh + s2r[hr, i]
        n_sub = S // per_dev
        for b in range(per_dev):
            blk = h * per_dev + b
            up = jnp.concatenate(
                [u2r[0, p, blk] + u2r[1, p, blk] for p in range(qpc)], axis=1
            )
            part = lax.dot_general(
                sh[b], up, (((0,), (0,)), ((), ())),
                preferred_element_type=jnp.float32,
            )
            base = fin[h, pl.ds(b * n_sub, n_sub)].reshape(n_sub * R, N)
            start = pl.multiple_of(h * (S * R) + b * BLOCK, BLOCK)
            obuf[hr, b] = (base + adapter_scale * part).astype(out.dtype)
            store = pltpu.make_async_copy(
                obuf.at[hr, b], out.at[pl.ds(start, BLOCK)], st_sem.at[hr, b]
            )
            store.start()
            stores.append(store)

    for store in stores:
        store.wait()

    def sent(ref, sem):
        rcopy(ref, ref, sem, dr.at[0], dev(0, 0, oc)).wait_send()

    for way in range(2):
        sent(tok.at[pl.ds(0, S), pl.ds(0, HX - 1), c], xs.at[way, 0])
        sent(tok.at[pl.ds(0, S), 0, c, :, pl.ds(0, half)], xs.at[way, 1])
        sent(sb.at[way, pl.ds(0, HY - 1)], ys.at[way, 0])
        sent(sb.at[way, HY - 1, :, pl.ds(0, R)], ys.at[way, 1])
    sent(tok.at[:, :, c], ds.at[0])
    sent(u1s.at[pl.ds(1, nx - 1)], u1ss.at[0])
    sent(u2s.at[pl.ds(1, ny - 1)], u2ss.at[1])

    @pl.when(dest_core != c)
    def _():
        u2_copy(0).wait_send()

    for hr in range(CORES):
        sent(s1s.at[hr, pl.ds(1 - hr, ny - 1 + hr)], s1ss.at[hr])
        sent(s2r.at[hr, pl.ds(1 - hr, nx - 1 + hr)], s2ss.at[hr])


def on_device(tokens, query_weight, down, up, ids, live, slots):
    nx = lax.axis_size("adapter") // CORES
    ny = lax.axis_size("tensor")
    rows, Fe = tokens.shape
    N = query_weight.shape[1]
    slots_dev, rank = down.shape[0], down.shape[1]
    R = rows // SUB
    NT = SUB + LX * (nx // 2)
    HX, HY = nx // 2, ny // 2
    lanes = N * CORES // ny
    qpc = N // lanes
    per_row = ids.shape[0] // ny
    per_dev = per_row // CORES
    bf = jnp.bfloat16
    dma = pltpu.SemaphoreType.DMA
    smem = pl.BlockSpec(memory_space=pltpu.SMEM)
    hbm = pl.BlockSpec(memory_space=pl.ANY)
    piece = (per_dev, rank, BLOCK)
    return pl.pallas_call(
        functools.partial(kernel, nx, ny),
        out_shape=jax.ShapeDtypeStruct((CORES * rows, N), bf),
        in_specs=[smem] * 3 + [hbm] * 4,
        out_specs=hbm,
        scratch_shapes=[
            pltpu.VMEM((NT, nx, CORES, R, Fe), bf),
            pltpu.VMEM((Fe, N), bf),
            pltpu.VMEM((slots_dev, rank, Fe), bf),
            pltpu.VMEM((nx, slots_dev, rank, lanes), bf),
            pltpu.VMEM((NT, nx, CORES * R, N), jnp.float32),
            pltpu.VMEM((2, HY, SUB, CORES * R, N), bf),
            pltpu.VMEM((2, HY, SUB, CORES * R, N), bf),
            pltpu.VMEM((CORES, SUB, R, N), jnp.float32),
            pltpu.VMEM((nx, SEATS, rank, lanes), bf),
            pltpu.VMEM((nx, SEATS, rank, lanes), bf),
            pltpu.VMEM((ny, per_row, rank, lanes), bf),
            pltpu.VMEM((CORES, qpc, per_row, rank, lanes), bf),
            pltpu.VMEM((SEATS, rank, BLOCK), bf),
            pltpu.VMEM((CORES, ny) + piece, bf),
            pltpu.VMEM((CORES, ny) + piece, bf),
            pltpu.VMEM(piece, bf),
            pltpu.VMEM((CORES, nx) + piece, bf),
            pltpu.SMEM((ids.shape[0],), jnp.int32),
            pltpu.SMEM((ids.shape[0],), jnp.int32),
            pltpu.SMEM((ids.shape[0],), jnp.int32),
            pltpu.VMEM((CORES, per_dev, BLOCK, N), bf),
            dma((CORES, per_dev)),
            dma((4,)),
            dma((2, 2)), dma((2, HX, SUB)),
            dma((1,)), dma((NT,)),
            dma((2, 2)), dma((2, HY, SUB)),
            dma((1,)), dma((1,)),
            dma((2,)), dma((CORES, qpc)),
            dma((CORES,)), dma((CORES,)),
            dma((CORES,)), dma((CORES,)),
        ],
        compiler_params=pltpu.CompilerParams(
            collective_id=0, has_side_effects=True,
            vmem_limit_bytes=60 * 1024 * 1024,
        ),
    )(ids, live, slots, tokens.reshape(SUB, R, Fe), query_weight, down, up)


def solution(mesh):
    placed = (
        P(("groups", "adapter"), "tensor"),
        P("tensor", "adapter"),
        P("adapter", None, "tensor"),
        P("adapter", None, None),
        P("groups"),
        P("groups"),
        P("groups"),
    )
    return jax.shard_map(
        on_device,
        mesh=mesh,
        in_specs=placed,
        out_specs=P(("groups", "tensor"), "adapter"),
        check_vma=False,
    )
```

time: 108 us -> 99.1 us (0.918)
  Pallas kernels: 106 us -> 96.1 us
    pallas_call x1, Pallas kernels: 106 us -> 96.1 us  [on_device(): pl.pallas_call(functools.partial(kernel, nx, ny), out_shape=jax.ShapeDtyp...]
where the time goes in v2:
time: 99.1 us; the launch traced here: 98 us
  Pallas kernels  96.1 us (97%)
  local copies, waits for them, and re-layouts  1.87 us (2%)
    pallas_call x1, Pallas kernels, on_device(): pl.pallas_call(functools.partial(kernel, nx, ny), out_shape=jax.ShapeDtyp...  96.1 us

profile of v2, /device:TPU:513, one launch (start us, length us, event | category | flops | bytes accessed | tf_op | source)
XLA Modules:
  0.0 98.0 jit_solution(13473654474675210366)
XLA Ops:
  0.0 96.1 %shard_map.73 = bf16[512,512]{1,0:T(8,128)(2,1)} custom-call(s32[32]{0:T(128)} %ids.1, s32[32]{0:T(128)} %live.1, s32[512]{0:T(512)} %slots.1, bf16[16,16,1024]{2,1,0:T(8,128)(2,1)} %bitcast.1, bf16[1024,512]{1,0:T(8,128)(2,1)} %w_h.1, bf16[32,16,1024]{2,1,0:T(8,128)(2,1)} %dn_h.1, bf16[32,16,8192]{2,1,0:T(8,128)(2,1)} %up_h.1), custom_call_target="tpu_custom_call" | custom-call | tf_op jit(solution)/shard_map/pallas_call | solution.py:434
  96.1 1.9 %copy.9 = bf16[512,512]{1,0:T(8,128)(2,1)} copy(bf16[512,512]{1,0:T(8,128)(2,1)} %shard_map.73) | data formatting | bytes 1048576

commit v3 on v2

--- a/solution.py
+++ b/solution.py
@@ -16,8 +16,8 @@
 LAG = 2
 AHEAD = 1
 SEATS = 4
-UP1 = 8
-UP2 = 20
+UP1 = 1
+UP2 = 6
 SH2 = 3
 adapter_scale = 2.0
 
@@ -81,9 +81,14 @@
         load_up(i).start()
 
     barrier = pltpu.get_barrier_semaphore()
-    for where in (dev(1), dev(-1), dev(0, 1), dev(0, -1), dev(0, 0, oc)):
-        pl.semaphore_signal(barrier, inc=1, device_id=where, device_id_type=MESH)
-    pl.semaphore_wait(barrier, 5)
+    peers = [(i, 0) for i in range(nx)] + [(0, i) for i in range(1, ny)]
+    for px, py in peers:
+        for core in (c, oc):
+            if px or py or core is oc:
+                pl.semaphore_signal(
+                    barrier, inc=1, device_id=dev(px, py, core), device_id_type=MESH
+                )
+    pl.semaphore_wait(barrier, CORES * len(peers) - 1)
 
     def x_copy(way, d, s):
         off = (nx - d) % nx if way == 0 else d
@@ -95,7 +100,7 @@
             cols = pl.ds(way * half, half)
             src, dst = src.at[:, cols], dst.at[:, cols]
         return rcopy(
-            src, dst, xs.at[way, 1 if d == HX - 1 else 0], xr.at[way, d, s],
+            src, dst, xs.at[way, 1 if d == HX - 1 else 0], xr.at[d, s],
             dev(1 if way == 0 else -1),
         )
 
@@ -112,7 +117,8 @@
         if d == HY:
             src, dst = src.at[pl.ds(0, R)], dst.at[pl.ds(0, R)]
         return rcopy(
-            src, dst, ys.at[way, 1 if d == HY else 0], yr.at[way, d - 1, s],
+            src, dst, ys.at[way, 1 if d == HY else 0],
+            yr.at[0 if d == 1 else d - 1 + way * (HY - 1), s],
             dev(0, 1 if way == 0 else -1),
         )
 
@@ -284,8 +290,8 @@
                 sb[way, d - 1, s] = (v[...] + got).astype(dt)
                 y_copy(way, d, s).start()
             else:
-                y_copy(0, 1, s).wait_recv()
-                y_copy(1, 1, s).wait_recv()
+                both = rb.at[:, 0, s]
+                rcopy(both, both, ys.at[0, 0], yr.at[0, s], dev(0, 1)).wait_recv()
                 total = (
                     v[...]
                     + rb[0, 0, s].astype(jnp.float32)
@@ -299,9 +305,10 @@
 
         @pl.when((s >= 0) & (s < S))
         def _():
-            for way in range(2):
-                x_copy(way, d - 1, s).wait_recv()
-                if d < HX:
+            both = tok.at[t, pl.ds(0, 1 if d == HX else 2), c]
+            rcopy(both, both, xs.at[0, 0], xr.at[d - 1, s], dev(1)).wait_recv()
+            if d < HX:
+                for way in range(2):
                     x_copy(way, d, s).start()
 
     def tick(t, carry):
@@ -460,9 +467,9 @@
             pltpu.VMEM((CORES, per_dev, BLOCK, N), bf),
             dma((CORES, per_dev)),
             dma((4,)),
-            dma((2, 2)), dma((2, HX, SUB)),
+            dma((2, 2)), dma((HX, SUB)),
             dma((1,)), dma((NT,)),
-            dma((2, 2)), dma((2, HY, SUB)),
+            dma((2, 2)), dma((2 * HY - 1, SUB)),
             dma((1,)), dma((1,)),
             dma((2,)), dma((CORES, qpc)),
             dma((CORES,)), dma((CORES,)),

time: 99.1 us -> 96.8 us (0.977)
  Pallas kernels: 96.1 us -> 94.7 us
    pallas_call x1, Pallas kernels: 96.1 us -> 94.7 us  [on_device(): pl.pallas_call(functools.partial(kernel, nx, ny), out_shape=jax.ShapeDtyp...]
where the time goes in v3:
time: 96.8 us; the launch traced here: 96.6 us
  Pallas kernels  94.7 us (98%)
  local copies, waits for them, and re-layouts  1.87 us (2%)
    pallas_call x1, Pallas kernels, on_device(): pl.pallas_call(functools.partial(kernel, nx, ny), out_shape=jax.ShapeDtyp...  94.7 us

profile of v3, /device:TPU:513, one launch (start us, length us, event | category | flops | bytes accessed | tf_op | source)
XLA Modules:
  0.0 96.6 jit_solution(14322445623571876401)
XLA Ops:
  0.0 94.7 %shard_map.73 = bf16[512,512]{1,0:T(8,128)(2,1)} custom-call(s32[32]{0:T(128)} %ids.1, s32[32]{0:T(128)} %live.1, s32[512]{0:T(512)} %slots.1, bf16[16,16,1024]{2,1,0:T(8,128)(2,1)} %bitcast.1, bf16[1024,512]{1,0:T(8,128)(2,1)} %w_h.1, bf16[32,16,1024]{2,1,0:T(8,128)(2,1)} %dn_h.1, bf16[32,16,8192]{2,1,0:T(8,128)(2,1)} %up_h.1), custom_call_target="tpu_custom_call" | custom-call | tf_op jit(solution)/shard_map/pallas_call | solution.py:441
  94.8 1.9 %copy.9 = bf16[512,512]{1,0:T(8,128)(2,1)} copy(bf16[512,512]{1,0:T(8,128)(2,1)} %shard_map.73) | data formatting | bytes 1048576

commit v4 on v3

--- a/solution.py
+++ b/solution.py
@@ -14,7 +14,7 @@
 LX = 2
 LY = 2
 LAG = 2
-AHEAD = 1
+AHEAD = 2
 SEATS = 4
 UP1 = 1
 UP2 = 6

time: 96.8 us -> 97.3 us (level)
  no operation moved by 1% of the time
where the time goes in v4:
time: 97.3 us; the launch traced here: 97.2 us
  Pallas kernels  95.3 us (98%)
  local copies, waits for them, and re-layouts  1.87 us (2%)
    pallas_call x1, Pallas kernels, on_device(): pl.pallas_call(functools.partial(kernel, nx, ny), out_shape=jax.ShapeDtyp...  95.3 us

profile of v4, /device:TPU:513, one launch (start us, length us, event | category | flops | bytes accessed | tf_op | source)
XLA Modules:
  0.0 97.2 jit_solution(8325319090859508985)
XLA Ops:
  0.0 95.3 %shard_map.73 = bf16[512,512]{1,0:T(8,128)(2,1)} custom-call(s32[32]{0:T(128)} %ids.1, s32[32]{0:T(128)} %live.1, s32[512]{0:T(512)} %slots.1, bf16[16,16,1024]{2,1,0:T(8,128)(2,1)} %bitcast.1, bf16[1024,512]{1,0:T(8,128)(2,1)} %w_h.1, bf16[32,16,1024]{2,1,0:T(8,128)(2,1)} %dn_h.1, bf16[32,16,8192]{2,1,0:T(8,128)(2,1)} %up_h.1), custom_call_target="tpu_custom_call" | custom-call | tf_op jit(solution)/shard_map/pallas_call | solution.py:441
  95.3 1.9 %copy.9 = bf16[512,512]{1,0:T(8,128)(2,1)} copy(bf16[512,512]{1,0:T(8,128)(2,1)} %shard_map.73) | data formatting | bytes 1048576
